TPU v7x, 8 devices: a whole 2x2x1 slice. The times are simulated.
8 devices in a mesh: batch: 1 (over z), seq_hi: 2 (over y), seq: 4 (over x, core).
Axes of the slice: x: 2, y: 2, z: 1, core: 2. Of those that a mesh axis runs over, the one named last changes fastest.
Arguments:
- x_seq: bfloat16 [24, 1536, 128], P('batch', ('seq_hi', 'seq'))
- w_f0: bfloat16 [2, 10, 128, 128], replicated
- w_f1: bfloat16 [2, 10, 128, 128], replicated
- w_g0: bfloat16 [2, 10, 128, 128], replicated
- w_g1: bfloat16 [2, 10, 128, 128], replicated
- w_res: bfloat16 [2, 10, 128, 128], replicated
- w_skip: bfloat16 [2, 10, 128, 128], replicated
Outputs:
- output 1: float32 [24, 1536, 128], P('batch', ('seq_hi', 'seq'))
- output 2: float32 [24, 1536, 128], P('batch', ('seq_hi', 'seq'))
All inputs are finite; a program needn't handle non-finite values.
Results may differ from a plain program's by a relative error of at most 0.00640755.
Values are sent between devices in bfloat16 or wider.
A program may use at most 1 GiB of HBM per device.

v0:
```python
import functools

import jax
import jax.numpy as jnp
from jax import lax
from jax.experimental import pallas as pl
from jax.experimental.pallas import tpu as pltpu
from jax.sharding import PartitionSpec as P

MESH = pl.DeviceIdType.MESH
SEQ_AXES = ("seq_hi", "seq")
N_DEV = 8
LAG = 2
F32 = jnp.float32
BF16 = jnp.bfloat16


def kernel(n_layers, n_cyc, blk, pad, x_ref, wf0, wf1, wg0, wg1, wr, ws, h_out, s_out,
           xbuf, wg_v, wo_v, ha0, hb0, ha1, hb1, ha2, hb2, hout_v, skip_v,
           w_sem, x_send, x_recv, o_send, h_recv, s_recv):
    hi, lo = lax.axis_index("seq_hi"), lax.axis_index("seq")
    me = hi * 4 + lo
    role = me // 2
    chan = x_ref.shape[-1]

    def dev(index):
        return {"seq_hi": index // 4, "seq": index % 4}

    w_copies = [
        pltpu.make_async_copy(wf1, wg_v.at[:, pl.ds(0, chan), pl.ds(0, chan)], w_sem.at[0]),
        pltpu.make_async_copy(wg1, wg_v.at[:, pl.ds(0, chan), pl.ds(chan, chan)], w_sem.at[1]),
        pltpu.make_async_copy(wf0, wg_v.at[:, pl.ds(chan, chan), pl.ds(0, chan)], w_sem.at[2]),
        pltpu.make_async_copy(wg0, wg_v.at[:, pl.ds(chan, chan), pl.ds(chan, chan)], w_sem.at[3]),
        pltpu.make_async_copy(wr, wo_v.at[:, :, pl.ds(0, chan)], w_sem.at[4]),
        pltpu.make_async_copy(ws, wo_v.at[:, :, pl.ds(chan, chan)], w_sem.at[5]),
    ]
    for copy in w_copies:
        copy.start()

    barrier = pltpu.get_barrier_semaphore()
    for other in range(N_DEV):
        @pl.when(me != other)
        def _():
            pl.semaphore_signal(barrier, inc=1, device_id=dev(other), device_id_type=MESH)
    pl.semaphore_wait(barrier, N_DEV - 1)

    def x_copies(act):
        def one(seq, target, q, unit):
            @pl.when(me == target)
            def _():
                act(pltpu.make_async_copy(x_ref.at[seq], xbuf.at[q, unit], x_recv.at[q]), True)

            @pl.when(me != target)
            def _():
                act(pltpu.make_async_remote_copy(
                    src_ref=x_ref.at[seq], dst_ref=xbuf.at[q, unit], send_sem=x_send, recv_sem=x_recv.at[q],
                    device_id=dev(target), device_id_type=MESH), False)

        for q in range(4):
            for target in range(2):
                if q < 2:
                    @pl.when(me < 4)
                    def _():
                        for half in range(2):
                            one(8 + 4 * target + 2 * q + half, target, q, half * 4 + me)
                else:
                    @pl.when(me < 2)
                    def _():
                        for part in range(4):
                            one(16 * target + 4 * (q - 2) + part, target, q, part * 2 + me)
            for target in range(2, N_DEV):
                one(4 * (target - 2) + q, target, q, me)

    x_copies(lambda copy, local: copy.start())

    def zero_pads(bufs, cps):
        for buf in bufs:
            for first in range(0, 8, cps):
                buf[pl.ds(first // cps * (pad + cps * blk), pad), :] = jnp.zeros((pad, chan), F32)

    @pl.when(role == 0)
    def _():
        zero_pads((ha1, hb1), 4)
        zero_pads((ha2, hb2), 2)

    @pl.when(role != 0)
    def _():
        zero_pads((ha0, hb0), 8)

    for copy in w_copies:
        copy.wait()

    def halve(l, carry):
        wg_v[l, :, pl.ds(chan, chan)] = wg_v[l, :, pl.ds(chan, chan)] * BF16(0.5)
        wo_v[l] = wo_v[l] * BF16(0.5)
        return carry

    lax.fori_loop(0, n_layers, halve, 0)

    def out_copies(act, q, unit, seq, target):
        for src, dst, recv in ((hout_v, h_out, h_recv), (skip_v, s_out, s_recv)):
            @pl.when(me == target)
            def _():
                act(pltpu.make_async_copy(src.at[q, unit], dst.at[seq], recv), True)

            @pl.when(me != target)
            def _():
                act(pltpu.make_async_remote_copy(
                    src_ref=src.at[q, unit], dst_ref=dst.at[seq], send_sem=o_send, recv_sem=recv,
                    device_id=dev(target), device_id_type=MESH), False)

    def outs_full(act, q):
        for unit in range(2, 8):
            if unit < 4:
                @pl.when(role != 2)
                def _():
                    out_copies(act, q, unit, 4 * (me - 2) + q, unit)
            else:
                out_copies(act, q, unit, 4 * (me - 2) + q, unit)

    def outs_pair(act, q):
        for unit in (2, 3, 6, 7, 0, 1, 4, 5):
            out_copies(act, q, unit, 8 + 4 * me + 2 * q + unit // 4, unit % 4)

    def outs_quad(act, q):
        for unit in range(8):
            out_copies(act, q, unit, 16 * me + 4 * (q - 2) + unit // 2, unit % 2)

    def compute():
        def sweep(q, cps, bufs):
            base = [k // cps * (pad + cps * blk) + pad + k % cps * blk for k in range(8)]

            pltpu.make_async_copy(xbuf.at[q], xbuf.at[q], x_recv.at[q]).wait()
            for k in range(8):
                bufs[0][pl.ds(base[k], blk), :] = xbuf[q, k].astype(F32)
                skip_v[q, k] = jnp.zeros((blk, chan), F32)

            def gates(l, dil, par, k):
                lhs = jnp.concatenate([bufs[par][pl.ds(base[k], blk), :], bufs[par][pl.ds(base[k] - dil, blk), :]], axis=1).astype(BF16)
                return jnp.dot(lhs, wg_v[l], preferred_element_type=F32)

            def activate(l, pre):
                act = (jnp.tanh(pre[:, :chan]) * (1.0 + jnp.tanh(pre[:, chan:]))).astype(BF16)
                return jnp.dot(act, wo_v[l], preferred_element_type=F32)

            def update(par, k, mixed):
                bufs[1 - par][pl.ds(base[k], blk), :] = bufs[par][pl.ds(base[k], blk), :] + mixed[:, :chan]
                skip_v[q, k] = skip_v[q, k] + mixed[:, chan:]

            def cycle(r, carry):
                steps = [(c, k) for c in range(n_cyc) for k in range(8)]
                pre, mixed = {}, {}
                for t in range(len(steps) + 2 * LAG):
                    if t < len(steps):
                        c, k = steps[t]
                        pre[t] = gates(r * n_cyc + c, 2**c, c % 2, k)
                    if 0 <= t - LAG < len(steps):
                        c, k = steps[t - LAG]
                        mixed[t - LAG] = activate(r * n_cyc + c, pre.pop(t - LAG))
                    if 0 <= t - 2 * LAG:
                        c, k = steps[t - 2 * LAG]
                        update(c % 2, k, mixed.pop(t - 2 * LAG))
                return carry

            lax.fori_loop(0, n_layers // n_cyc, cycle, 0)
            for k in range(8):
                hout_v[q, k] = bufs[0][pl.ds(base[k], blk), :]

        @pl.when(role == 0)
        def _():
            @pl.loop(0, 2)
            def _(q):
                sweep(q, 4, (ha1, hb1))
                outs_pair(lambda copy, local: copy.start(), q)

            @pl.loop(2, 4)
            def _(q):
                sweep(q, 2, (ha2, hb2))
                outs_quad(lambda copy, local: copy.start(), q)

        @pl.when(role != 0)
        def _():
            @pl.loop(0, 4)
            def _(q):
                sweep(q, 8, (ha0, hb0))
                outs_full(lambda copy, local: copy.start(), q)

    compute()

    def sent(copy, local):
        if not local:
            copy.wait_send()

    x_copies(sent)

    @pl.when(role == 0)
    def _():
        @pl.loop(0, 2)
        def _(q):
            outs_pair(sent, q)

        @pl.loop(2, 4)
        def _(q):
            outs_quad(sent, q)

    @pl.when(role != 0)
    def _():
        @pl.loop(0, 4)
        def _(q):
            outs_full(sent, q)

    pltpu.make_async_copy(h_out, h_out, h_recv).wait()
    pltpu.make_async_copy(s_out, s_out, s_recv).wait()


def solution(mesh):
    seq_spec = P("batch", SEQ_AXES, None)

    def local_stack(x_loc, w_f0, w_f1, w_g0, w_g1, w_res, w_skip):
        n_rep, n_cyc, chan = w_f0.shape[:3]
        n_layers = n_rep * n_cyc
        n_seq, blk, _ = x_loc.shape
        pad = 2 ** (n_cyc - 1)
        weights = [w.reshape(n_layers, chan, chan) for w in (w_f0, w_f1, w_g0, w_g1, w_res, w_skip)]
        any_spec = pl.BlockSpec(memory_space=pl.ANY)
        out = jax.ShapeDtypeStruct((n_seq, blk, chan), F32)
        return pl.pallas_call(
            functools.partial(kernel, n_layers, n_cyc, blk, pad),
            out_shape=(out, out),
            in_specs=[any_spec] * 7,
            out_specs=(any_spec, any_spec),
            scratch_shapes=[
                pltpu.VMEM((4, 8, blk, chan), BF16),
                pltpu.VMEM((n_layers, 2 * chan, 2 * chan), BF16),
                pltpu.VMEM((n_layers, chan, 2 * chan), BF16),
                pltpu.VMEM((pad + 8 * blk, chan), F32),
                pltpu.VMEM((pad + 8 * blk, chan), F32),
                pltpu.VMEM((2 * pad + 8 * blk, chan), F32),
                pltpu.VMEM((2 * pad + 8 * blk, chan), F32),
                pltpu.VMEM((4 * pad + 8 * blk, chan), F32),
                pltpu.VMEM((4 * pad + 8 * blk, chan), F32),
                pltpu.VMEM((4, 8, blk, chan), F32),
                pltpu.VMEM((4, 8, blk, chan), F32),
                pltpu.SemaphoreType.DMA((6,)),
                pltpu.SemaphoreType.DMA,
                pltpu.SemaphoreType.DMA((4,)),
                pltpu.SemaphoreType.DMA,
                pltpu.SemaphoreType.DMA,
                pltpu.SemaphoreType.DMA,
            ],
            compiler_params=pltpu.CompilerParams(collective_id=0, has_side_effects=True, vmem_limit_bytes=60 * 2**20),
        )(x_loc, *weights)

    return jax.shard_map(local_stack, mesh=mesh, in_specs=(seq_spec, P(), P(), P(), P(), P(), P()), out_specs=(seq_spec, seq_spec), check_vma=False)
```

profile of v0, /device:TPU:5, one launch (start us, length us, event | category | flops | bytes accessed | tf_op | source)
XLA Modules:
  0.0 60.7 jit_solution(11095721153042757619)
XLA Ops:
  0.6 55.1 %shard_map.86 = (f32[24,192,128]{2,1,0:T(8,128)}, f32[24,192,128]{2,1,0:T(8,128)}) custom-call(bf16[24,192,128]{2,1,0:T(8,128)(2,1)} %x_ref.1, bf16[20,128,128]{2,1,0:T(8,128)(2,1)} %bitcast.6, bf16[20,128,128]{2,1,0:T(8,128)(2,1)} %bitcast.7, bf16[20,128,128]{2,1,0:T(8,128)(2,1)} %bitcast.8, bf16[20,128,128]{2,1,0:T(8,128)(2,1)} %bitcast.9, ...), custom_call_target="tpu_custom_call" | custom-call | tf_op jit(solution)/shard_map/pallas_call | solution.py:227
  55.8 0.0 copy-start
  55.8 3.4 %copy.11 = f32[24,192,128]{2,1,0:T(8,128)} copy(f32[24,192,128]{2,1,0:T(8,128)} %get-tuple-element.4) | data formatting | bytes 4718592
  59.2 0.0 copy-done
  59.2 1.4 %copy.12 = f32[24,192,128]{2,1,0:T(8,128)} copy(f32[24,192,128]{2,1,0:T(8,128)S(1)} %copy-done) | data formatting | bytes 4718592
Async XLA Ops:
  55.8 3.5 %copy-start = (f32[24,192,128]{2,1,0:T(8,128)S(1)}, f32[24,192,128]{2,1,0:T(8,128)}, u32[]{:S(2)}) copy-start(f32[24,192,128]{2,1,0:T(8,128)} %get-tuple-element.5) | copy-start | bytes 7077892
where the time goes:
time: 61.5 us; the launch traced here: 60.7 us
  Pallas kernels  55.1 us (90%)
  local copies, waits for them, and re-layouts  4.86 us (8%)
  between operations  0.65 us (1%)
    pallas_call x1, Pallas kernels, local_stack(): pl.pallas_call(functools.partial(kernel, n_layers, n_cyc, blk, pad), out_...  55.1 us
    unnamed x4, local copies, waits for them, and re-layouts  4.86 us

commit v1 on v0

--- a/solution.py
+++ b/solution.py
@@ -10,6 +10,7 @@
 MESH = pl.DeviceIdType.MESH
 SEQ_AXES = ("seq_hi", "seq")
 N_DEV = 8
+PIECES = 4
 LAG = 2
 F32 = jnp.float32
 BF16 = jnp.bfloat16
@@ -97,34 +98,35 @@
 
     lax.fori_loop(0, n_layers, halve, 0)
 
-    def out_copies(act, q, unit, seq, target):
+    def out_copies(act, start, q, unit, seq, target):
         for src, dst, recv in ((hout_v, h_out, h_recv), (skip_v, s_out, s_recv)):
             @pl.when(me == target)
             def _():
-                act(pltpu.make_async_copy(src.at[q, unit], dst.at[seq], recv), True)
+                if start:
+                    dst[seq] = src[q, unit]
 
             @pl.when(me != target)
             def _():
                 act(pltpu.make_async_remote_copy(
                     src_ref=src.at[q, unit], dst_ref=dst.at[seq], send_sem=o_send, recv_sem=recv,
-                    device_id=dev(target), device_id_type=MESH), False)
-
-    def outs_full(act, q):
+                    device_id=dev(target), device_id_type=MESH))
+
+    def outs_full(act, start, q):
         for unit in range(2, 8):
             if unit < 4:
                 @pl.when(role != 2)
                 def _():
-                    out_copies(act, q, unit, 4 * (me - 2) + q, unit)
+                    out_copies(act, start, q, unit, 4 * (me - 2) + q, unit)
             else:
-                out_copies(act, q, unit, 4 * (me - 2) + q, unit)
-
-    def outs_pair(act, q):
+                out_copies(act, start, q, unit, 4 * (me - 2) + q, unit)
+
+    def outs_pair(act, start, q):
         for unit in (2, 3, 6, 7, 0, 1, 4, 5):
-            out_copies(act, q, unit, 8 + 4 * me + 2 * q + unit // 4, unit % 4)
-
-    def outs_quad(act, q):
+            out_copies(act, start, q, unit, 8 + 4 * me + 2 * q + unit // 4, unit % 4)
+
+    def outs_quad(act, start, q):
         for unit in range(8):
-            out_copies(act, q, unit, 16 * me + 4 * (q - 2) + unit // 2, unit % 2)
+            out_copies(act, start, q, unit, 16 * me + 4 * (q - 2) + unit // 2, unit % 2)
 
     def compute():
         def sweep(q, cps, bufs):
@@ -171,19 +173,19 @@
             @pl.loop(0, 2)
             def _(q):
                 sweep(q, 4, (ha1, hb1))
-                outs_pair(lambda copy, local: copy.start(), q)
+                outs_pair(lambda copy: copy.start(), True, q)
 
             @pl.loop(2, 4)
             def _(q):
                 sweep(q, 2, (ha2, hb2))
-                outs_quad(lambda copy, local: copy.start(), q)
+                outs_quad(lambda copy: copy.start(), True, q)
 
         @pl.when(role != 0)
         def _():
             @pl.loop(0, 4)
             def _(q):
                 sweep(q, 8, (ha0, hb0))
-                outs_full(lambda copy, local: copy.start(), q)
+                outs_full(lambda copy: copy.start(), True, q)
 
     compute()
 
@@ -197,20 +199,43 @@
     def _():
         @pl.loop(0, 2)
         def _(q):
-            outs_pair(sent, q)
+            outs_pair(lambda copy: copy.wait_send(), False, q)
 
         @pl.loop(2, 4)
         def _(q):
-            outs_quad(sent, q)
+            outs_quad(lambda copy: copy.wait_send(), False, q)
 
     @pl.when(role != 0)
     def _():
         @pl.loop(0, 4)
         def _(q):
-            outs_full(sent, q)
-
-    pltpu.make_async_copy(h_out, h_out, h_recv).wait()
-    pltpu.make_async_copy(s_out, s_out, s_recv).wait()
+            outs_full(lambda copy: copy.wait_send(), False, q)
+
+    def arrived(count):
+        for dst, recv in ((h_out, h_recv), (s_out, s_recv)):
+            part = dst.at[pl.ds(0, count)]
+            pltpu.make_async_copy(part, part, recv).wait()
+
+    @pl.when(role == 0)
+    def _():
+        arrived(12)
+
+    @pl.when(role != 0)
+    def _():
+        arrived(20)
+
+
+def to_hbm(h_vmem, s_vmem, h_hbm, s_hbm, sems):
+    piece = h_vmem.shape[0] // PIECES
+    copies = []
+    for i in range(PIECES):
+        rows = pl.ds(i * piece, piece)
+        for j, (src, dst) in enumerate(((h_vmem, h_hbm), (s_vmem, s_hbm))):
+            copies.append(pltpu.make_async_copy(src.at[rows], dst.at[rows], sems.at[j, i]))
+    for copy in copies:
+        copy.start()
+    for copy in copies:
+        copy.wait()
 
 
 def solution(mesh):
@@ -224,11 +249,13 @@
         weights = [w.reshape(n_layers, chan, chan) for w in (w_f0, w_f1, w_g0, w_g1, w_res, w_skip)]
         any_spec = pl.BlockSpec(memory_space=pl.ANY)
         out = jax.ShapeDtypeStruct((n_seq, blk, chan), F32)
-        return pl.pallas_call(
+        vmem_spec = pl.BlockSpec(memory_space=pltpu.VMEM)
+        vmem_out = pltpu.VMEM((n_seq, blk, chan), F32)
+        landed = pl.pallas_call(
             functools.partial(kernel, n_layers, n_cyc, blk, pad),
-            out_shape=(out, out),
-            in_specs=[any_spec] * 7,
-            out_specs=(any_spec, any_spec),
+            out_shape=(vmem_out, vmem_out),
+            in_specs=[pl.BlockSpec(memory_space=pltpu.HBM)] * 7,
+            out_specs=(vmem_spec, vmem_spec),
             scratch_shapes=[
                 pltpu.VMEM((4, 8, blk, chan), BF16),
                 pltpu.VMEM((n_layers, 2 * chan, 2 * chan), BF16),
@@ -248,7 +275,15 @@
                 pltpu.SemaphoreType.DMA,
                 pltpu.SemaphoreType.DMA,
             ],
-            compiler_params=pltpu.CompilerParams(collective_id=0, has_side_effects=True, vmem_limit_bytes=60 * 2**20),
-        )(x_loc, *weights)
+            compiler_params=pltpu.CompilerParams(collective_id=0, has_side_effects=True, vmem_limit_bytes=40 * 2**20),
+        )(*[pltpu.with_memory_space_constraint(v, pltpu.HBM) for v in (x_loc, *weights)])
+        return pl.pallas_call(
+            to_hbm,
+            out_shape=(out, out),
+            in_specs=[vmem_spec, vmem_spec],
+            out_specs=(any_spec, any_spec),
+            scratch_shapes=[pltpu.SemaphoreType.DMA((2, PIECES))],
+            compiler_params=pltpu.CompilerParams(vmem_limit_bytes=2 * 2**20),
+        )(*landed)
 
     return jax.shard_map(local_stack, mesh=mesh, in_specs=(seq_spec, P(), P(), P(), P(), P(), P()), out_specs=(seq_spec, seq_spec), check_vma=False)

time: 61.5 us -> 59.2 us (0.963)
  local copies, waits for them, and re-layouts: 4.86 us -> 0 us
  Pallas kernels: 55.1 us -> 57.6 us
    unnamed x4 -> x0, local copies, waits for them, and re-layouts: 4.86 us -> none
    pallas_call x0 -> x1, Pallas kernels: none -> 2.24 us  [local_stack(): pl.pallas_call(to_hbm, out_shape=(out, out), in_specs=[vmem_spec, vmem_sp...]
where the time goes in v1:
time: 59.2 us; the launch traced here: 58.4 us
  Pallas kernels  57.6 us (97%)
  between operations  0.8 us (1%)
    pallas_call x1, Pallas kernels, local_stack(): pl.pallas_call(functools.partial(kernel, n_layers, n_cyc, blk, pad), out_...  55.3 us
    pallas_call x1, Pallas kernels, local_stack(): pl.pallas_call(to_hbm, out_shape=(out, out), in_specs=[vmem_spec, vmem_sp...  2.24 us

profile of v1, /device:TPU:5, one launch (start us, length us, event | category | flops | bytes accessed | tf_op | source)
XLA Modules:
  0.0 58.4 jit_solution(11891014313701334509)
XLA Ops:
  0.6 55.3 %shard_map.86 = (f32[24,192,128]{2,1,0:T(8,128)S(1)}, f32[24,192,128]{2,1,0:T(8,128)S(1)}) custom-call(bf16[24,192,128]{2,1,0:T(8,128)(2,1)} %x_ref.1, bf16[20,128,128]{2,1,0:T(8,128)(2,1)} %bitcast.6, bf16[20,128,128]{2,1,0:T(8,128)(2,1)} %bitcast.7, bf16[20,128,128]{2,1,0:T(8,128)(2,1)} %bitcast.8, bf16[20,128,128]{2,1,0:T(8,128)(2,1)} %bitcast.9, ...), custom_call_target="tpu_custom_call" | custom-call | tf_op jit(solution)/shard_map/pallas_call | solution.py:254
  56.0 2.2 %shard_map.87 = (f32[24,192,128]{2,1,0:T(8,128)}, f32[24,192,128]{2,1,0:T(8,128)}) custom-call(f32[24,192,128]{2,1,0:T(8,128)S(1)} %get-tuple-element.4.h_vmem, f32[24,192,128]{2,1,0:T(8,128)S(1)} %get-tuple-element.5.s_vmem), custom_call_target="tpu_custom_call" | custom-call | tf_op jit(solution)/shard_map/pallas_call | solution.py:280
